TPU v7x, 32 devices: a whole 2x2x4 slice. The times are simulated.
32 devices in a mesh: lat: 8 (over y, x, core), lon: 4 (over z).
Axes of the slice: x: 2, y: 2, z: 4, core: 2. Of those that a mesh axis runs over, the one named last changes fastest.
Arguments:
- coeffs_old: float32 [640, 2, 3, 50, 640], P(('lat', 'lon')), may hold values from -0.16 to 0.16
- noise: bfloat16 [640, 2, 3, 50, 640], P(('lat', 'lon')), may hold values from -6 to 6
- legendre: float32 [640, 640, 640], P(('lat', 'lon')), may hold values from -0.25 to 0.25
- decay: float32 [3], replicated, may hold values from 0.3 to 0.97
- amplitude: float32 [3, 640], replicated, may hold values from 0.005 to 0.05
- wavenumber_of_slot: int32 [640], replicated, may hold values from 0 to 639, as said below
- lat_order: int32 [640], replicated, may hold values from 0 to 639, each once
Outputs:
- coeffs_new: float32 [640, 2, 3, 50, 640], P(('lat', 'lon'))
- pattern: float32 [640, 50, 1280], P(('lat', 'lon'))
Inputs may be any that keep to these rules, and one draw needn't show every extreme that they name: `wavenumber_of_slot`: every wavenumber fills exactly one slot; the sums of the wavenumbers of one device's 20 slots differ between devices by less than 32. `lat_order`: every latitude stands in exactly one row.
All inputs are finite; a program needn't handle non-finite values.
Results may differ from a plain program's by a relative error of at most 0.0003.
Values sent between devices are 32-bit elements; how exact they have to be, the bound alone decides.
A program may use at most 192 MiB of HBM per device.

v0:
```python
import jax
import jax.numpy as jnp
from jax import lax
from jax.sharding import PartitionSpec as P

LON = 1280
TWO_PI = 6.283185307179586


def evolve(coeffs_old, noise, decay, amplitude, waves):
    width = coeffs_old.shape[4]
    offsets = lax.broadcasted_iota(jnp.int32, (waves.shape[0], width), 1)
    live = waves[:, None] + offsets < width
    padded = jnp.concatenate([amplitude, jnp.zeros_like(amplitude)], axis=1)
    spread = jax.vmap(lambda wave: lax.dynamic_slice_in_dim(padded, wave, width, 1))(waves)
    factor = jnp.sqrt(1.0 - decay * decay)
    fresh = decay[None, None, :, None, None] * coeffs_old + (spread * factor[None, :, None])[
        :, None, :, None, :
    ] * noise.astype(jnp.float32)
    return jnp.where(live[:, None, None, None, :], fresh, jnp.zeros_like(fresh))


def synthesis_table(waves, length):
    column = lax.broadcasted_iota(jnp.int32, (waves.shape[0], length), 1)
    phase = waves[:, None] * column % length
    angle = phase.astype(jnp.float32) * (TWO_PI / length)
    weight = jnp.where(waves == 0, 1.0, 2.0).astype(jnp.float32)[:, None]
    return jnp.stack([weight * jnp.cos(angle), -weight * jnp.sin(angle)], axis=1)


def synthesize(values, table):
    return jnp.einsum("sreq,srl->qel", values, table, precision=lax.Precision.HIGHEST)


def local(coeffs_old, noise, legendre, decay, amplitude, wavenumber_of_slot, lat_order):
    lat_count = lax.axis_size("lat")
    lon_count = lax.axis_size("lon")
    lat_index = lax.axis_index("lat")
    lon_index = lax.axis_index("lon")
    slots = coeffs_old.shape[0]
    mine = lax.dynamic_slice_in_dim(
        wavenumber_of_slot, (lat_index * lon_count + lon_index) * slots, slots
    )
    coeffs_new = evolve(coeffs_old, noise, decay, amplitude, mine)
    field = jnp.einsum("srkej,slj->srel", coeffs_new, legendre, precision=lax.Precision.HIGHEST)
    field = jnp.take(field, lat_order, axis=3)
    ordered = wavenumber_of_slot.reshape(lat_count, lon_count, slots).transpose(1, 0, 2).reshape(-1)
    full_table = synthesis_table(ordered, LON)
    pattern = synthesize(
        lax.all_to_all(
            lax.all_to_all(field, "lat", split_axis=3, concat_axis=0, tiled=True),
            "lon",
            split_axis=3,
            concat_axis=0,
            tiled=True,
        ),
        full_table,
    )
    return (coeffs_new, pattern)


def solution(mesh):
    in_specs = (
        P(("lat", "lon"), None, None, None, None),
        P(("lat", "lon"), None, None, None, None),
        P(("lat", "lon"), None, None),
        P(),
        P(),
        P(),
        P(),
    )
    out_specs = (P(("lat", "lon"), None, None, None, None), P(("lat", "lon"), None, None))
    return jax.shard_map(local, mesh=mesh, in_specs=in_specs, out_specs=out_specs, check_vma=False)
```

profile of v0, /device:TPU:0, one launch (start us, length us, event | category | flops | bytes accessed | tf_op | source)
XLA Modules:
  0.0 590.6 jit_solution(11389839738425668350)
XLA Ops:
  0.6 0.7 compare_select_fusion
  1.3 0.7 compare_and_fusion
  2.0 0.8 fusion.12
  2.8 0.7 concatenate.6
  3.5 26.4 %while.1 = (s32[]{:T(128)}, f32[3,1280]{1,0:T(4,128)S(1)}, s32[20,2]{0,1:T(2,128)S(1)}, f32[20,3,640]{2,1,0:T(4,128)S(1)}, s32[]{:T(128)}) while((s32[]{:T(128)}, f32[3,1280]{1,0:T(4,128)S(1)}, s32[20,2]{0,1:T(2,128)S(1)}, f32[20,3,640]{2,1,0:T(4,128)S(1)}, s32[]{:T(128)}) %tuple.24), condition=%wide.while_cond, body=%wide.while_body.sunk | while | flops 2 | bytes 20585 | solution.py:15
  4.1 0.7 bitcast_dynamic-update-slice_fusion.2
  5.4 0.7 bitcast_dynamic-update-slice_fusion.2
  6.2 0.5 slice.14
  6.7 0.7 bitcast_dynamic-update-slice_fusion.2
  7.5 0.5 slice.14
  8.1 0.7 bitcast_dynamic-update-slice_fusion.2
  8.9 0.5 slice.14
  9.4 0.7 bitcast_dynamic-update-slice_fusion.2
  10.7 0.7 bitcast_dynamic-update-slice_fusion.2
  12.0 0.7 bitcast_dynamic-update-slice_fusion.2
  13.3 0.7 bitcast_dynamic-update-slice_fusion.2
  14.7 0.7 bitcast_dynamic-update-slice_fusion.2
  16.0 0.7 bitcast_dynamic-update-slice_fusion.2
  17.3 0.7 bitcast_dynamic-update-slice_fusion.2
  18.6 0.7 bitcast_dynamic-update-slice_fusion.2
  19.9 0.7 bitcast_dynamic-update-slice_fusion.2
  21.2 0.7 bitcast_dynamic-update-slice_fusion.2
  22.6 0.7 bitcast_dynamic-update-slice_fusion.2
  23.9 0.7 bitcast_dynamic-update-slice_fusion.2
  25.2 0.7 bitcast_dynamic-update-slice_fusion.2
  26.5 0.7 bitcast_dynamic-update-slice_fusion.2
  27.8 0.7 bitcast_dynamic-update-slice_fusion.2
  29.2 0.7 bitcast_dynamic-update-slice_fusion.2
  29.9 0.7 subtract_sqrt_fusion
  30.8 32.2 %fusion.15 = (f32[20,2,50,640]{3,1,2,0:T(2,128)}, f32[20,2,3,50,640]{4,1,3,2,0:T(2,128)}) fusion(bf16[20,2,3,50,640]{4,1,3,2,0:T(2,128)(2,1)} %param.8, f32[20,3,640]{2,1,0:T(4,128)S(1)} %broadcast_multiply_fusion, f32[20,2,3,50,640]{4,1,3,2,0:T(2,128)} %param.7, f32[3]{0:T(128)} %param.10, pred[20,640]{1,0:T(8,128)(4,1)S(1)} %add_compare_fusion), kind=kLoop, calls=%fused_computation.33 | loop fusion | flops 21760000 | bytes 43686412 | tf_op jit(solution)/shard_map/srkej,slj->srel/reduce_sum | solution.py:45
  63.0 36.1 %fusion = f32[20,2,50,640]{3,2,1,0:T(8,128)} fusion(f32[20,640,640]{2,1,0:T(8,128)} %param.9, f32[20,2,50,640]{3,1,2,0:T(2,128)} %get-tuple-element.18), kind=kOutput, calls=%fused_computation.3 | convolution fusion | flops 9830400000 | bytes 43008000 | tf_op jit(solution)/shard_map/srkej,slj->srel/dot_general | solution.py:45
  99.1 15.9 %copy.33 = f32[20,2,50,640]{2,1,3,0:T(2,128)} copy(f32[20,2,50,640]{3,2,1,0:T(8,128)} %fusion) | data formatting | bytes 10240000 | tf_op jit(solution)/shard_map/srkej,slj->srel/dot_general | solution.py:45
  115.0 38.6 %gather_fusion = f32[640,20,2,50]{3,2,1,0:T(2,128)} fusion(f32[20,2,50,640]{2,1,3,0:T(2,128)} %copy.33, s32[1024]{0:T(1024)S(1)} %pad_clamp_fusion), kind=kCustom, calls=%fused_computation | custom fusion | bytes 10242560 | tf_op jit(solution)/shard_map/jit(_take)/gather | solution.py:46
  153.6 10.2 %fusion.16 = f32[640,20,2,50]{3,2,1,0:T(2,128)} fusion(f32[640,20,2,50]{3,2,1,0:T(2,128)} %gather_fusion, pred[640]{0:T(1024)(128)(4,1)S(1)} %compare_and_fusion), kind=kLoop, calls=%fused_computation.34 | loop fusion | flops 1280000 | bytes 10240640
  163.8 27.8 %reshape.218 = f32[8,1,160000]{2,1,0:T(1,128)} reshape(f32[640,20,2,50]{3,2,1,0:T(2,128)} %fusion.16) | data formatting | bytes 10240000
  191.5 64.3 %all_to_all.36 = f32[8,1,160000]{2,1,0:T(1,128)} all-to-all(f32[8,1,160000]{2,1,0:T(1,128)} %reshape.218), channel_id=1, replica_groups=mesh['lat'=8,'lon'=4] {'lat'}, dimensions={0} | all-to-all | bytes 10240000 | tf_op jit(solution)/shard_map/all_to_all | solution.py:51
  255.8 0.5 broadcast.203
  256.3 17.0 %reduce = f32[8,160000]{1,0:T(8,128)} reduce(f32[8,1,160000]{2,1,0:T(1,128)} %all_to_all.36, f32[]{:T(128)} %broadcast.203), dimensions={1}, to_apply=%all_to_all.26.reduce_sub_computation | reduce | bytes 10240004 | tf_op jit(solution)/shard_map/all_to_all | solution.py:51
  273.3 33.3 %reshape.219 = f32[640,20,2,50]{3,2,1,0:T(2,128)} reshape(f32[8,160000]{1,0:T(8,128)} %reduce) | data formatting | bytes 10240000
  306.6 17.1 %copy.42 = f32[20,2,50,8,80]{4,3,1,2,0:T(8,128)} copy(f32[20,2,50,8,80]{2,1,0,4,3:T(2,128)} %bitcast.41) | data formatting | bytes 10240000 | tf_op jit(solution)/shard_map/all_to_all | solution.py:51
  323.7 13.0 %copy.35 = f32[8,20,2,50,80]{4,2,3,1,0:T(2,128)} copy(f32[8,20,2,50,80]{4,0,2,3,1:T(8,128)} %bitcast.43) | data formatting | bytes 10240000 | tf_op jit(solution)/shard_map/all_to_all | solution.py:51
  336.7 18.0 %copy.36 = f32[160,2,50,80]{0,1,2,3:T(2,128)} copy(f32[160,2,50,80]{3,1,2,0:T(2,128)} %bitcast.42) | data formatting | bytes 10240000 | tf_op jit(solution)/shard_map/all_to_all | solution.py:51
  354.7 5.7 all-to-all-start.1
  360.7 15.2 %cosine_multiply_fusion = (f32[640,1,1280]{2,0,1:T(8,128)S(1)}, f32[640,1,1280]{2,0,1:T(8,128)}) fusion(s32[640]{0:T(1024)S(1)} %reshape.185, f32[640]{0:T(1024)S(1)} %get-tuple-element.24, f32[640]{0:T(1024)S(1)} %get-tuple-element.25), kind=kLoop, calls=%fused_computation.17 | loop fusion | flops 9011200 | bytes 6561280 | tf_op jit(solution)/shard_map/mul | solution.py:28
  375.9 164.0 %all-to-all-done.1 = f32[160,2,50,80]{0,1,2,3:T(2,128)} async-done(((f32[160,2,50,80]{0,1,2,3:T(2,128)}), f32[160,2,50,80]{0,1,2,3:T(2,128)}, u32[]{:S(2)}, u32[]{:S(2)}) %all-to-all-start.1) | async-done | bytes 5120032 | tf_op jit(solution)/shard_map/all_to_all | solution.py:50
  539.9 11.8 %copy.44 = f32[4,160,2,50,20]{1,0,3,2,4:T(4,128)} copy(f32[4,160,2,50,20]{1,2,3,4,0:T(2,128)} %bitcast.11) | data formatting | bytes 10240000 | tf_op jit(solution)/shard_map/all_to_all | solution.py:50
  551.7 9.5 %reshape.217 = f32[640,2,50,20]{0,2,1,3:T(8,128)} reshape(f32[4,160,2,50,20]{1,0,3,2,4:T(4,128)} %copy.44) | data formatting | bytes 10240000 | tf_op jit(solution)/shard_map/all_to_all | solution.py:50
  561.3 29.1 %fusion.6 = f32[20,50,1280]{2,1,0:T(8,128)} fusion(f32[640,2,50,20]{0,2,1,3:T(8,128)} %reshape.217, f32[640,1,1280]{2,0,1:T(8,128)} %get-tuple-element.23, f32[640,1,1280]{2,0,1:T(8,128)S(1)} %get-tuple-element.22), kind=kOutput, calls=%fused_computation.13 | convolution fusion | flops 19662438400 | bytes 16793600 | tf_op jit(solution)/shard_map/sreq,srl->qel/dot_general | solution.py:32
  (48 shorter events, 10.7 us)
Async XLA Ops:
  354.7 5.8 copy-start
  354.7 185.2 %all-to-all-start.1 = ((f32[160,2,50,80]{0,1,2,3:T(2,128)}), f32[160,2,50,80]{0,1,2,3:T(2,128)}, u32[]{:S(2)}, u32[]{:S(2)}) async-start(f32[160,2,50,80]{0,1,2,3:T(2,128)} %copy.36), calls=%async_computation.1 | async-start | bytes 16384000 | tf_op jit(solution)/shard_map/all_to_all | solution.py:50
where the time goes:
time: 601 us; the launch traced here: 591 us
  local copies, waits for them, and re-layouts  213 us (35%)
  waiting for transfers between devices  164 us (27%)
  other arithmetic  77.6 us (13%)
  matrix products  65.2 us (11%)
  blocking collectives  64.3 us (11%)
    all_to_all x1, waiting for transfers between devices, local(): lax.all_to_all(lax.all_to_all(field, 'lat', split_axis=3, concat_axis=0,...  164 us
    all_to_all x1, blocking collectives, local(): lax.all_to_all(field, 'lat', split_axis=3, concat_axis=0, tiled=True)  64.3 us
    unnamed x4, local copies, waits for them, and re-layouts  61.1 us
    all_to_all x4, local copies, waits for them, and re-layouts, local(): lax.all_to_all(field, 'lat', split_axis=3, concat_axis=0, tiled=True)  48.6 us
    gather x1, local copies, waits for them, and re-layouts, local(): field = jnp.take(field, lat_order, axis=3)  38.6 us
    dot_general x1, matrix products, local(): jnp.einsum('srkej,slj->srel', coeffs_new, legendre, precision=lax.Precisi...  36.1 us
    reduce_sum x1, other arithmetic, local(): jnp.einsum('srkej,slj->srel', coeffs_new, legendre, precision=lax.Precisi...  32.2 us
    dot_general x1, matrix products, synthesize(): jnp.einsum('sreq,srl->qel', values, table, precision=lax.Precision.HIGHEST)  29.1 us
  transfers between devices with their start and end apart: 1, of which 1 were waited for; matrix products, arithmetic and copies ran while one was open for 3% of the time, Pallas kernels for 0%

commit v1 on v0

--- a/solution.py
+++ b/solution.py
@@ -5,6 +5,22 @@
 
 LON = 1280
 TWO_PI = 6.283185307179586
+
+
+def exchange_in_pairs(shard, axis, split, join):
+    ways, here = (lax.axis_size(axis), lax.axis_index(axis))
+    width = shard.shape[split] // ways
+    shape = list(shard.shape)
+    shape[split] = width
+    height = shape[join]
+    shape[join] = height * ways
+    full = jnp.zeros(shape, shard.dtype)
+    for mask in range(ways):
+        part = lax.dynamic_slice_in_dim(shard, (here ^ mask) * width, width, axis=split)
+        if mask:
+            part = lax.ppermute(part, axis, [(d, d ^ mask) for d in range(ways)])
+        full = lax.dynamic_update_slice_in_dim(full, part, (here ^ mask) * height, axis=join)
+    return full
 
 
 def evolve(coeffs_old, noise, decay, amplitude, waves):
@@ -47,12 +63,8 @@
     ordered = wavenumber_of_slot.reshape(lat_count, lon_count, slots).transpose(1, 0, 2).reshape(-1)
     full_table = synthesis_table(ordered, LON)
     pattern = synthesize(
-        lax.all_to_all(
-            lax.all_to_all(field, "lat", split_axis=3, concat_axis=0, tiled=True),
-            "lon",
-            split_axis=3,
-            concat_axis=0,
-            tiled=True,
+        exchange_in_pairs(
+            lax.all_to_all(field, "lat", split_axis=3, concat_axis=0, tiled=True), "lon", 3, 0
         ),
         full_table,
     )

time: 601 us -> 638 us (1.062)
  the two profiles are of different devices: /device:TPU:0 before, /device:TPU:18 now
where the time goes in v1:
time: 638 us; the launch traced here: 627 us
  local copies, waits for them, and re-layouts  327 us (51%)
  waiting for transfers between devices  144 us (23%)
  other arithmetic  78.1 us (12%)
  matrix products  68.2 us (11%)
  starting transfers between devices  8.54 us (1%)
    dynamic_slice x5, local copies, waits for them, and re-layouts, exchange_in_pairs(): lax.dynamic_slice_in_dim(shard, (here ^ mask) * width, width, axis=split)  87.4 us
    ppermute x3, waiting for transfers between devices, exchange_in_pairs(): part = lax.ppermute(part, axis, [(d, d ^ mask) for d in range(ways)])  86.5 us
    unnamed x4, local copies, waits for them, and re-layouts  61.3 us
    all_to_all x1, waiting for transfers between devices, local(): lax.all_to_all(field, 'lat', split_axis=3, concat_axis=0, tiled=True)  57.6 us
    dynamic_update_slice x4, local copies, waits for them, and re-layouts, exchange_in_pairs(): lax.dynamic_update_slice_in_dim(full, part, (here ^ mask) * height, axis=...  56.9 us
    gather x1, local copies, waits for them, and re-layouts, local(): field = jnp.take(field, lat_order, axis=3)  38.6 us
    dot_general x1, matrix products, local(): jnp.einsum('srkej,slj->srel', coeffs_new, legendre, precision=lax.Precisi...  36.1 us
    reduce_sum x1, other arithmetic, local(): jnp.einsum('srkej,slj->srel', coeffs_new, legendre, precision=lax.Precisi...  32.3 us
  transfers between devices with their start and end apart: 4, of which 3 were waited for; matrix products, arithmetic and copies ran while one was open for 16% of the time, Pallas kernels for 0%

profile of v1, /device:TPU:18, one launch (start us, length us, event | category | flops | bytes accessed | tf_op | source)
XLA Modules:
  0.0 626.6 jit_solution(9082055295321734505)
XLA Ops:
  2.0 0.8 fusion.12
  3.5 26.4 %while.1 = (s32[]{:T(128)}, f32[3,1280]{1,0:T(4,128)S(1)}, s32[20,2]{0,1:T(2,128)S(1)}, f32[20,3,640]{2,1,0:T(4,128)S(1)}, s32[]{:T(128)}) while((s32[]{:T(128)}, f32[3,1280]{1,0:T(4,128)S(1)}, s32[20,2]{0,1:T(2,128)S(1)}, f32[20,3,640]{2,1,0:T(4,128)S(1)}, s32[]{:T(128)}) %tuple.27), condition=%wide.while_cond, body=%wide.while_body.sunk | while | flops 2 | bytes 20577 | solution.py:31
  4.1 0.7 bitcast_dynamic-update-slice_fusion.2
  5.4 0.7 bitcast_dynamic-update-slice_fusion.2
  6.7 0.7 bitcast_dynamic-update-slice_fusion.2
  8.1 0.7 bitcast_dynamic-update-slice_fusion.2
  9.4 0.7 bitcast_dynamic-update-slice_fusion.2
  10.7 0.7 bitcast_dynamic-update-slice_fusion.2
  12.0 0.7 bitcast_dynamic-update-slice_fusion.2
  13.3 0.7 bitcast_dynamic-update-slice_fusion.2
  14.7 0.7 bitcast_dynamic-update-slice_fusion.2
  16.0 0.7 bitcast_dynamic-update-slice_fusion.2
  17.3 0.7 bitcast_dynamic-update-slice_fusion.2
  18.6 0.7 bitcast_dynamic-update-slice_fusion.2
  19.9 0.7 bitcast_dynamic-update-slice_fusion.2
  21.2 0.7 bitcast_dynamic-update-slice_fusion.2
  22.6 0.7 bitcast_dynamic-update-slice_fusion.2
  30.8 32.3 %fusion.15 = (f32[20,2,50,640]{3,1,2,0:T(2,128)}, f32[20,2,3,50,640]{4,1,3,2,0:T(2,128)}) fusion(bf16[20,2,3,50,640]{4,1,3,2,0:T(2,128)(2,1)} %param.8, f32[20,3,640]{2,1,0:T(4,128)S(1)} %broadcast_multiply_fusion, f32[20,2,3,50,640]{4,1,3,2,0:T(2,128)} %param.7, f32[3]{0:T(128)} %param.10, pred[20,640]{1,0:T(8,128)(4,1)S(1)} %add_compare_fusion), kind=kLoop, calls=%fused_computation.37 | loop fusion | flops 21760000 | bytes 43686412 | tf_op jit(solution)/shard_map/srkej,slj->srel/reduce_sum | solution.py:61
  63.0 36.1 %fusion = f32[20,2,50,640]{3,2,1,0:T(8,128)} fusion(f32[20,640,640]{2,1,0:T(8,128)} %param.9, f32[20,2,50,640]{3,1,2,0:T(2,128)} %get-tuple-element.18), kind=kOutput, calls=%fused_computation.3 | convolution fusion | flops 9830400000 | bytes 43008000 | tf_op jit(solution)/shard_map/srkej,slj->srel/dot_general | solution.py:61
  99.1 15.9 %copy.27 = f32[20,2,50,640]{2,1,3,0:T(2,128)} copy(f32[20,2,50,640]{3,2,1,0:T(8,128)} %fusion) | data formatting | bytes 10240000 | tf_op jit(solution)/shard_map/srkej,slj->srel/dot_general | solution.py:61
  115.0 38.6 %gather_fusion = f32[640,20,2,50]{3,2,1,0:T(2,128)} fusion(f32[20,2,50,640]{2,1,3,0:T(2,128)} %copy.27, s32[1024]{0:T(1024)S(1)} %pad_clamp_fusion), kind=kCustom, calls=%fused_computation | custom fusion | bytes 10242560 | tf_op jit(solution)/shard_map/jit(_take)/gather | solution.py:62
  153.6 10.2 %fusion.16 = f32[640,20,2,50]{3,2,1,0:T(2,128)} fusion(f32[640,20,2,50]{3,2,1,0:T(2,128)} %gather_fusion, pred[640]{0:T(1024)(128)(4,1)S(1)} %compare_and_fusion), kind=kLoop, calls=%fused_computation.38 | loop fusion | flops 1280000 | bytes 10240640
  163.8 27.8 %reshape.217 = f32[8,1,160000]{2,1,0:T(1,128)} reshape(f32[640,20,2,50]{3,2,1,0:T(2,128)} %fusion.16) | data formatting | bytes 10240000
  191.5 5.1 all-to-all-start
  196.6 57.6 %all-to-all-done = f32[8,1,160000]{2,1,0:T(1,128)} async-done(((f32[8,1,160000]{2,1,0:T(1,128)}), f32[8,1,160000]{2,1,0:T(1,128)}, u32[]{:S(2)}, u32[]{:S(2)}) %all-to-all-start) | async-done | bytes 5120032 | tf_op jit(solution)/shard_map/all_to_all | solution.py:67
  254.7 16.8 %reduce = f32[8,160000]{1,0:T(8,128)} reduce(f32[8,1,160000]{2,1,0:T(1,128)} %all-to-all-done, f32[]{:T(128)} %broadcast.203), dimensions={1}, to_apply=%all_to_all.13.reduce_sub_computation | reduce | bytes 10240004 | tf_op jit(solution)/shard_map/all_to_all | solution.py:67
  271.5 33.5 %reshape.218 = f32[640,20,2,50]{3,2,1,0:T(2,128)} reshape(f32[8,160000]{1,0:T(8,128)} %reduce) | data formatting | bytes 10240000
  305.0 17.1 %copy.39 = f32[20,2,50,8,80]{4,3,1,2,0:T(8,128)} copy(f32[20,2,50,8,80]{2,1,0,4,3:T(2,128)} %bitcast.37) | data formatting | bytes 10240000 | tf_op jit(solution)/shard_map/all_to_all | solution.py:67
  322.1 12.0 %copy.29 = f32[8,20,2,50,80]{4,2,3,1,0:T(2,128)S(1)} copy(f32[8,20,2,50,80]{4,0,2,3,1:T(8,128)} %bitcast.38) | data formatting | bytes 10240000 | tf_op jit(solution)/shard_map/all_to_all | solution.py:67
  334.1 36.3 %constant_dynamic-slice_fusion.1 = (f32[160,2,50,20]{3,1,2,0:T(2,128)}, f32[160,2,50,20]{3,1,2,0:T(2,128)}, f32[160,2,50,20]{3,1,2,0:T(2,128)}, f32[160,2,50,20]{3,1,2,0:T(2,128)}) fusion(f32[160,2,50,80]{3,1,2,0:T(2,128)S(1)} %bitcast.36, s32[]{:T(128)S(6)} %select_n.85, s32[]{:T(128)S(6)} %select_n.83, s32[]{:T(128)S(6)} %select_n.81, s32[]{:T(128)S(6)} %select_n.79), kind=kLoop, calls=%fused_computation.29 | loop fusion | bytes 10240016 | tf_op jit(solution)/shard_map/dynamic_slice | solution.py:19
  370.4 13.1 %copy.31 = f32[160,2,50,20]{0,1,3,2:T(2,128)} copy(f32[160,2,50,20]{3,1,2,0:T(2,128)} %get-tuple-element.24) | data formatting | bytes 2560000 | tf_op jit(solution)/shard_map/dynamic_slice | solution.py:19
  383.4 1.6 collective-permute-start
  385.0 13.0 %copy.33 = f32[160,2,50,20]{0,1,3,2:T(2,128)} copy(f32[160,2,50,20]{3,1,2,0:T(2,128)} %get-tuple-element.23) | data formatting | bytes 2560000 | tf_op jit(solution)/shard_map/dynamic_slice | solution.py:19
  398.4 13.1 %copy.35 = f32[160,2,50,20]{0,1,3,2:T(2,128)} copy(f32[160,2,50,20]{3,1,2,0:T(2,128)} %get-tuple-element.22) | data formatting | bytes 2560000 | tf_op jit(solution)/shard_map/dynamic_slice | solution.py:19
  411.5 1.6 collective-permute-start.2
  413.3 15.9 %cosine_multiply_fusion = (f32[640,1,1280]{2,0,1:T(8,128)}, f32[640,1,1280]{2,0,1:T(8,128)}) fusion(s32[640]{0:T(1024)S(1)} %reshape.185, f32[640]{0:T(1024)S(1)} %get-tuple-element.28, f32[640]{0:T(1024)S(1)} %get-tuple-element.29), kind=kLoop, calls=%fused_computation.17 | loop fusion | flops 9011200 | bytes 6561280 | tf_op jit(solution)/shard_map/mul | solution.py:44
  429.2 12.0 %copy.30 = f32[160,2,50,20]{0,2,1,3:T(8,128)S(1)} copy(f32[160,2,50,20]{3,1,2,0:T(2,128)} %get-tuple-element.25) | data formatting | bytes 2560000 | tf_op jit(solution)/shard_map/dynamic_slice | solution.py:19
  441.2 2.9 broadcast_in_dim.49
  444.1 15.8 %dynamic_update_slice.12 = f32[640,2,50,20]{0,2,1,3:T(8,128)} dynamic-update-slice(f32[640,2,50,20]{0,2,1,3:T(8,128)} %broadcast_in_dim.49, f32[160,2,50,20]{0,2,1,3:T(8,128)S(1)} %copy.30, s32[]{:T(128)S(6)} %select_n.80, s32[]{:T(128)} %constant.24.clone.1, s32[]{:T(128)} %constant.24.clone.1, s32[]{:T(128)} %constant.24.clone.1) | dynamic-update-slice | bytes 2560004 | tf_op jit(solution)/shard_map/dynamic_update_slice | solution.py:22
  459.9 2.2 copy.32
  462.1 15.0 %dynamic_update_slice.13 = f32[640,2,50,20]{0,2,1,3:T(8,128)} dynamic-update-slice(f32[640,2,50,20]{0,2,1,3:T(8,128)} %dynamic_update_slice.12, f32[160,2,50,20]{0,2,1,3:T(8,128)S(1)} %copy.32, s32[]{:T(128)S(6)} %select_n.82, s32[]{:T(128)} %constant.24.clone.1, s32[]{:T(128)} %constant.24.clone.1, s32[]{:T(128)} %constant.24.clone.1) | dynamic-update-slice | bytes 2560004 | tf_op jit(solution)/shard_map/dynamic_update_slice | solution.py:22
  477.1 54.4 %collective-permute-done.1 = f32[160,2,50,20]{0,1,3,2:T(2,128)} collective-permute-done((f32[160,2,50,20]{0,1,3,2:T(2,128)}, f32[160,2,50,20]{0,1,3,2:T(2,128)}, u32[]{:S(2)}, u32[]{:S(2)}) %collective-permute-start.1) | collective-permute-done | bytes 1280032 | tf_op jit(solution)/shard_map/ppermute | solution.py:21
  531.5 2.2 copy.34
  533.7 10.4 %dynamic_update_slice.14 = f32[640,2,50,20]{0,2,1,3:T(8,128)} dynamic-update-slice(f32[640,2,50,20]{0,2,1,3:T(8,128)} %dynamic_update_slice.13, f32[160,2,50,20]{0,2,1,3:T(8,128)S(1)} %copy.34, s32[]{:T(128)S(6)} %select_n.84, s32[]{:T(128)} %constant.24.clone.1, s32[]{:T(128)} %constant.24.clone.1, s32[]{:T(128)} %constant.24.clone.1) | dynamic-update-slice | bytes 2560004 | tf_op jit(solution)/shard_map/dynamic_update_slice | solution.py:22
  544.1 32.1 %collective-permute-done.2 = f32[160,2,50,20]{0,1,3,2:T(2,128)} collective-permute-done((f32[160,2,50,20]{0,1,3,2:T(2,128)}, f32[160,2,50,20]{0,1,3,2:T(2,128)}, u32[]{:S(2)}, u32[]{:S(2)}) %collective-permute-start.2) | collective-permute-done | bytes 1280032 | tf_op jit(solution)/shard_map/ppermute | solution.py:21
  576.2 2.2 copy.36
  578.5 15.8 %dynamic_update_slice.15 = f32[640,2,50,20]{0,2,1,3:T(8,128)} dynamic-update-slice(f32[640,2,50,20]{0,2,1,3:T(8,128)} %dynamic_update_slice.14, f32[160,2,50,20]{0,2,1,3:T(8,128)S(1)} %copy.36, s32[]{:T(128)S(6)} %select_n.86, s32[]{:T(128)} %constant.24.clone.1, s32[]{:T(128)} %constant.24.clone.1, s32[]{:T(128)} %constant.24.clone.1) | dynamic-update-slice | bytes 2560004 | tf_op jit(solution)/shard_map/dynamic_update_slice | solution.py:22
  594.3 32.1 %fusion.6 = f32[20,50,1280]{2,1,0:T(8,128)} fusion(f32[640,2,50,20]{0,2,1,3:T(8,128)} %dynamic_update_slice.15, f32[640,1,1280]{2,0,1:T(8,128)} %get-tuple-element.27, f32[640,1,1280]{2,0,1:T(8,128)} %get-tuple-element.26), kind=kOutput, calls=%fused_computation.13 | convolution fusion | flops 19662438400 | bytes 16793600 | tf_op jit(solution)/shard_map/sreq,srl->qel/dot_general | solution.py:48
  (63 shorter events, 19.5 us)
Async XLA Ops:
  191.5 62.7 %all-to-all-start = ((f32[8,1,160000]{2,1,0:T(1,128)}), f32[8,1,160000]{2,1,0:T(1,128)}, u32[]{:S(2)}, u32[]{:S(2)}) async-start(f32[8,1,160000]{2,1,0:T(1,128)} %reshape.217), calls=%async_computation | async-start | bytes 10240000 | tf_op jit(solution)/shard_map/all_to_all | solution.py:67
  383.4 76.4 %collective-permute-start = (f32[160,2,50,20]{0,1,3,2:T(2,128)}, f32[160,2,50,20]{0,1,3,2:T(2,128)}, u32[]{:S(2)}, u32[]{:S(2)}) collective-permute-start(f32[160,2,50,20]{0,1,3,2:T(2,128)} %copy.31), channel_id=1, source_target_pairs={{0,1},{1,0},{2,3},{3,2},{4,5},{5,4},{6,7},{7,6},{8,9},{9,8},{10,11... | collective-permute-start | bytes 3840008 | tf_op jit(solution)/shard_map/ppermute | solution.py:21
  398.1 15.0 %copy-start = (s32[640]{0:T(1024)S(1)}, s32[640]{0:T(1024)}, u32[]{:S(2)}) copy-start(s32[640]{0:T(1024)} %param.12) | copy-start | bytes 7684
  398.1 133.4 %collective-permute-start.1 = (f32[160,2,50,20]{0,1,3,2:T(2,128)}, f32[160,2,50,20]{0,1,3,2:T(2,128)}, u32[]{:S(2)}, u32[]{:S(2)}) collective-permute-start(f32[160,2,50,20]{0,1,3,2:T(2,128)} %copy.33), channel_id=1, source_target_pairs={{0,2},{1,3},{2,0},{3,1},{4,6},{5,7},{6,4},{7,5},{8,10},{9,11},{10,... | collective-permute-start | bytes 3840008 | tf_op jit(solution)/shard_map/ppermute | solution.py:21
  411.5 164.8 %collective-permute-start.2 = (f32[160,2,50,20]{0,1,3,2:T(2,128)}, f32[160,2,50,20]{0,1,3,2:T(2,128)}, u32[]{:S(2)}, u32[]{:S(2)}) collective-permute-start(f32[160,2,50,20]{0,1,3,2:T(2,128)} %copy.35), channel_id=1, source_target_pairs={{0,3},{1,2},{2,1},{3,0},{4,7},{5,6},{6,5},{7,4},{8,11},{9,10},{10,... | collective-permute-start | bytes 3840008 | tf_op jit(solution)/shard_map/ppermute | solution.py:21
